TPU v7x, 32 devices: a whole 2x2x4 slice. The times are simulated.
32 devices in a mesh: row: 4 (over x, core), col: 8 (over z, y).
Axes of the slice: x: 2, y: 2, z: 4, core: 2. Of those that a mesh axis runs over, the one named last changes fastest.
Arguments:
- hamiltonian: bfloat16 [2912, 2912], P('row', 'col'), may hold values from -6 to 6
- new_atom: int32 [224], replicated, may hold values from 0 to 223, as said below
- pattern: int32 [224, 224], P('row', 'col'), may hold values 0 or 1
Outputs:
- sign_matrix: float32 [2912, 2912], P('row', 'col')
Inputs may be any that keep to these rules, and one draw needn't show every extreme that they name: `new_atom`: each old atom appears once. Block column b holds atoms b * 28 to (b + 1) * 28 - 1 in both orders. For each new block column d and each v from 0 to 27, exactly one atom of new block column d comes from old block column (d - 1 - (v mod 8)) mod 8, so the number of atoms that old block column b sends to new block column (b + k) mod 8 is the number of such v with (1 + v) mod 8 = k.
All inputs are finite; a program needn't handle non-finite values. No bound on the sum of `pattern` on one device may be relied on, other than what follows from the above.
Results may differ from a plain program's by a relative error of at most 0.0029.
Values may be sent and summed in bfloat16 or wider, within the bound.
A program may use at most 64 MiB of HBM per device.

v0:
```python
import jax
import jax.numpy as jnp
from jax import lax
from jax.sharding import PartitionSpec as P

NBF = 13
BF = jnp.bfloat16
F32 = jnp.float32


def mm(a, b):
    return jnp.dot(a, b, preferred_element_type=F32)


def spread(n):
    i = lax.broadcasted_iota(jnp.int32, (n * NBF, n), 0)
    a = lax.broadcasted_iota(jnp.int32, (n * NBF, n), 1) * NBF
    return (i >= a) & (i < a + NBF)


def on_device(hamiltonian, new_atom, pattern):
    rows_here, cols_here = hamiltonian.shape
    order = rows_here * lax.axis_size("row")
    atoms = order // NBF
    ar, ac = pattern.shape
    row_here = lax.axis_index("row")
    col_here = lax.axis_index("col")
    panel = lax.all_gather(hamiltonian, "col", axis=1, tiled=True)
    pat = lax.all_gather(pattern.astype(BF), ("row", "col"), axis=0, tiled=False)
    n_row, n_col = (lax.axis_size("row"), lax.axis_size("col"))
    pat = pat.reshape(n_row, n_col, ar, ac).transpose(0, 2, 1, 3).reshape(atoms, atoms)
    old = jnp.arange(atoms, dtype=jnp.int32)
    perm = (new_atom[:, None] == old[None, :]).astype(BF)
    mine = (new_atom[None, :] == row_here * ar + jnp.arange(ar, dtype=jnp.int32)[:, None]).astype(
        BF
    )
    pat_rows = mm(mine, pat).astype(BF)
    e_row = spread(ar)
    e_col = spread(ac)
    e_rowb = e_row.astype(BF)
    rows_masked = mm(e_rowb, mm(pat_rows, perm).astype(BF)).astype(BF)
    keep = mm(rows_masked, spread(atoms).astype(BF).T).astype(BF)
    m = panel * keep
    total = lax.psum(jnp.sum(m.astype(F32) ** 2), "row")
    s = lax.rsqrt(total / order)

    def old_index(n, here, e):
        mine_atoms = lax.dynamic_slice_in_dim(new_atom, here * n, n)
        base = jnp.sum(
            jnp.where(e, (mine_atoms - jnp.arange(n, dtype=jnp.int32))[None, :], 0), axis=1
        )
        return base * NBF + jnp.arange(n * NBF, dtype=jnp.int32)

    full = jnp.arange(order, dtype=jnp.int32)
    pick_col = (full[:, None] == old_index(ac, col_here, e_col)[None, :]).astype(BF)
    pick_row = (old_index(ar, row_here, e_row)[:, None] == full[None, :]).astype(BF)
    right = lax.all_gather(mm(m, pick_col).astype(BF), "row", axis=0, tiled=True)
    e_colt = e_col.astype(BF).T
    here_cols = lax.dynamic_slice_in_dim(pat_rows, col_here * ac, ac, axis=1)
    keep_sq = mm(mm(e_rowb, here_cols).astype(BF), e_colt)
    square = (mm(m, right) * (s * s) * keep_sq).astype(BF)
    square = lax.all_gather(square, "row", axis=0, tiled=True)
    cube = lax.all_gather((mm(m, square) * s).astype(BF), "row", axis=0, tiled=True)
    start = (mm(pick_row, right) * s).astype(BF).astype(F32)
    keep_out = mm(mm(e_rowb, pattern.astype(BF)).astype(BF), e_colt)
    return keep_out * (1.5 * start - 0.5 * mm(pick_row, cube))


def solution(mesh):
    in_specs = (P("row", "col"), P(), P("row", "col"))
    out_specs = P("row", "col")
    return jax.shard_map(
        on_device, mesh=mesh, in_specs=in_specs, out_specs=out_specs, check_vma=False
    )
```

profile of v0, /device:TPU:0, one launch (start us, length us, event | category | flops | bytes accessed | tf_op | source)
XLA Modules:
  0.0 211.8 jit_solution(7994260219636314159)
XLA Ops:
  6.5 0.7 all-gather.14.cloned.1.call-update
  7.3 0.7 convert_bitcast_fusion
  8.0 75.1 %all-gather.2 = bf16[32,56,28]{1,2,0:T(8,128)(2,1)S(1)} all-gather(bf16[1,56,28]{1,2,0:T(8,128)(2,1)S(1)} %convert_bitcast_fusion), channel_id=2, replica_groups=mesh['row'=4,'col'=8] {'row','col'}, dimensions={0}, use_global_device_ids=true | all-gather | bytes 103488 | tf_op jit(solution)/shard_map/all_gather | solution.py:29
  83.2 0.2 copy.12
  83.3 0.2 reshape.30
  83.5 0.8 iota_subtract_fusion
  84.4 0.9 convolution_convert_fusion.5
  85.3 0.9 convolution_convert_fusion.4
  86.2 5.0 %all-gather.14.cloned.1.call-done = bf16[8,364,728]{1,2,0:T(8,128)(2,1)} async-done(((bf16[1,364,728]{1,2,0:T(8,128)(2,1)}), bf16[8,364,728]{1,2,0:T(8,128)(2,1)}) %all-gather.14.cloned.1.call-update) | async-done | bytes 4239888 | tf_op jit(solution)/shard_map/all_gather | solution.py:28
  91.2 4.9 %copy.9 = bf16[8,364,728]{1,0,2:T(8,128)(2,1)} copy(bf16[8,364,728]{1,2,0:T(8,128)(2,1)} %all-gather.14.cloned.1.call-done) | data formatting | bytes 8479744 | tf_op jit(solution)/shard_map/all_gather | solution.py:28
  96.1 8.6 %reshape.34 = bf16[2912,728]{0,1:T(8,128)(2,1)} reshape(bf16[8,364,728]{1,0,2:T(8,128)(2,1)} %copy.9) | data formatting | bytes 8479744
  104.7 6.9 %multiply_reduce_fusion = (f32[]{:T(128)}, bf16[728,2912]{1,0:T(8,128)(2,1)}) fusion(s32[224]{0:T(256)S(1)} %get-tuple-element.8, s32[224]{0:T(256)S(1)} %get-tuple-element.7, bf16[56,224]{1,0:T(8,128)(2,1)S(1)} %convolution_convert_fusion.4, s32[56]{0:T(128)S(1)} %get-tuple-element.10, s32[56]{0:T(128)S(1)} %get-tuple-element.9, bf16[2912,728]{0,1:T(8,128)(2,1)} %reshape.34), kind=kOutput, calls=%fused_computation | convolution fusion | flops 987197120 | bytes 8507076 | tf_op jit(solution)/shard_map/dot_general | solution.py:12
  111.6 5.5 %fusion.19 = bf16[728,364]{1,0:T(8,128)(2,1)} fusion(bf16[728,2912]{1,0:T(8,128)(2,1)} %get-tuple-element.6, s32[364]{0:T(512)S(1)} %iota_add_fusion.1), kind=kOutput, calls=%fused_computation.28 | convolution fusion | flops 1544638336 | bytes 4771312 | tf_op jit(solution)/shard_map/dot_general | solution.py:12
  117.2 6.2 %psum.7 = f32[]{:T(128)} all-reduce(f32[]{:T(128)} %get-tuple-element.5), channel_id=1, replica_groups=mesh['row'=4,'col'=8] {'row'}, use_global_device_ids=true, to_apply=%region_3.4 | all-reduce | flops 1 | bytes 8 | tf_op jit(solution)/shard_map/psum | solution.py:44
  124.2 15.2 %all-gather.8.cloned.1.call-done = bf16[2912,364]{1,0:T(8,128)(2,1)} async-done(((bf16[728,364]{1,0:T(8,128)(2,1)}), bf16[2912,364]{1,0:T(8,128)(2,1)}) %all-gather.8.cloned.1.call-update) | async-done | bytes 2119952 | tf_op jit(solution)/shard_map/all_gather | solution.py:57
  139.3 5.4 %convolution_multiply_fusion.1 = f32[728,364]{1,0:T(8,128)S(1)} fusion(bf16[728,2912]{1,0:T(8,128)(2,1)} %get-tuple-element.6, bf16[2912,364]{1,0:T(8,128)(2,1)} %all-gather.8.cloned.1.call-done, f32[]{:T(128)S(6)} %mul.104), kind=kOutput, calls=%fused_computation.17 | convolution fusion | flops 1543578368 | bytes 7419780 | tf_op jit(solution)/shard_map/dot_general | solution.py:12
  144.7 1.5 fusion.17
  146.2 0.2 all-gather.12.cloned.1.call-start
  146.5 23.3 %all-gather.10.cloned.1.call-done = bf16[2912,364]{1,0:T(8,128)(2,1)} async-done(((bf16[728,364]{1,0:T(8,128)(2,1)}), bf16[2912,364]{1,0:T(8,128)(2,1)}) %all-gather.10.cloned.1.call-update) | async-done | bytes 2119952 | tf_op jit(solution)/shard_map/all_gather | solution.py:62
  169.7 6.2 %fusion.18 = bf16[728,364]{1,0:T(8,128)(2,1)} fusion(bf16[728,2912]{1,0:T(8,128)(2,1)} %get-tuple-element.6, bf16[2912,364]{1,0:T(8,128)(2,1)} %all-gather.10.cloned.1.call-done, f32[]{:T(128)S(6)} %rsqrt.3), kind=kOutput, calls=%fused_computation.27 | convolution fusion | flops 1543843328 | bytes 6889796 | tf_op jit(solution)/shard_map/dot_general | solution.py:12
  176.2 2.5 %fusion.16 = f32[728,364]{1,0:T(8,128)S(1)} fusion(bf16[2912,364]{1,0:T(8,128)(2,1)S(1)} %copy-done.2, s32[728]{0:T(1024)S(1)} %iota_add_fusion, f32[]{:T(128)S(6)} %rsqrt.3), kind=kOutput, calls=%fused_computation.25 | convolution fusion | flops 1546493184 | bytes 3182820 | tf_op jit(solution)/shard_map/dot_general | solution.py:12
  178.7 20.7 %all-gather.12.cloned.1.call-done = bf16[2912,364]{1,0:T(8,128)(2,1)} async-done(((bf16[728,364]{1,0:T(8,128)(2,1)}), bf16[2912,364]{1,0:T(8,128)(2,1)}) %all-gather.12.cloned.1.call-update) | async-done | bytes 2119952 | tf_op jit(solution)/shard_map/all_gather | solution.py:63
  199.5 4.1 %fusion.13 = f32[728,364]{1,0:T(8,128)S(1)} fusion(f32[728,364]{1,0:T(8,128)S(1)} %fusion.16, bf16[2912,364]{1,0:T(8,128)(2,1)} %all-gather.12.cloned.1.call-done, s32[728]{0:T(1024)S(1)} %iota_add_fusion), kind=kOutput, calls=%fused_computation.22 | convolution fusion | flops 1545963264 | bytes 4242784 | tf_op jit(solution)/shard_map/dot_general | solution.py:12
  203.6 1.6 convolution_multiply_fusion.3
  (21 shorter events, 0.5 us)
Async XLA Ops:
  6.5 84.7 %all-gather.14.cloned.1.call-start = ((), (), s32[]{:S(2)}) async-start(), calls=%async_computation.3 | async-start | bytes 5031936 | tf_op jit(solution)/shard_map/all_gather | solution.py:28
  7.3 132.1 %all-gather.8.cloned.1.call-start = ((), (), s32[]{:S(2)}) async-start(), calls=%async_computation | async-start | bytes 2795520 | tf_op jit(solution)/shard_map/all_gather | solution.py:57
  117.1 52.6 %all-gather.10.cloned.1.call-start = ((), (), s32[]{:S(2)}) async-start(), calls=%async_computation.1 | async-start | bytes 2795520 | tf_op jit(solution)/shard_map/all_gather | solution.py:62
  146.2 29.8 %copy-start.1 = (s32[224]{0:T(256)S(1)}, s32[224]{0:T(256)}, u32[]{:S(2)}) copy-start(s32[224]{0:T(256)} %param.4) | copy-start | bytes 2692
  146.2 30.0 %copy-start.2 = (bf16[2912,364]{1,0:T(8,128)(2,1)S(1)}, bf16[2912,364]{1,0:T(8,128)(2,1)}, u32[]{:S(2)}) copy-start(bf16[2912,364]{1,0:T(8,128)(2,1)} %all-gather.8.cloned.1.call-done) | copy-start | bytes 6359812
  146.2 53.2 %all-gather.12.cloned.1.call-start = ((), (), s32[]{:S(2)}) async-start(), calls=%async_computation.2 | async-start | bytes 2795520 | tf_op jit(solution)/shard_map/all_gather | solution.py:63
  178.7 24.9 %copy-start = (s32[56,28]{0,1:T(8,128)S(1)}, s32[56,28]{0,1:T(8,128)}, u32[]{:S(2)}) copy-start(s32[56,28]{0,1:T(8,128)} %param.5) | copy-start | bytes 18820
Sparse Core Ops, SparseCore 0:
  9.5 81.6 all-gather.13
  117.2 22.0 all-gather.7
  146.3 23.3 all-gather.9
  176.1 23.3 all-gather.11
where the time goes:
time: 212 us
  blocking collectives  81.4 us (38%)
  waiting for transfers between devices  64.9 us (31%)
  matrix products  35.5 us (17%)
  between operations  14 us (7%)
  local copies, waits for them, and re-layouts  13.8 us (7%)
    all_gather x1, blocking collectives, on_device(): lax.all_gather(pattern.astype(BF), ('row', 'col'), axis=0, tiled=False)  75.1 us
    dot_general x10, matrix products, mm(): return jnp.dot(a, b, preferred_element_type=F32)  35.5 us
    all_gather x1, waiting for transfers between devices, on_device(): square = lax.all_gather(square, 'row', axis=0, tiled=True)  23.3 us
    all_gather x1, waiting for transfers between devices, on_device(): lax.all_gather((mm(m, square) * s).astype(BF), 'row', axis=0, tiled=True)  20.7 us
    all_gather x1, waiting for transfers between devices, on_device(): lax.all_gather(mm(m, pick_col).astype(BF), 'row', axis=0, tiled=True)  15.2 us
    unnamed x7, local copies, waits for them, and re-layouts  8.62 us
    psum x1, blocking collectives, on_device(): total = lax.psum(jnp.sum(m.astype(F32) ** 2), 'row')  6.25 us
    all_gather x1, waiting for transfers between devices, on_device(): panel = lax.all_gather(hamiltonian, 'col', axis=1, tiled=True)  5 us
  transfers between devices with their start and end apart: 4, of which 4 were waited for; matrix products, arithmetic and copies ran while one was open for 3% of the time, Pallas kernels for 0%

commit v1 on v0

--- a/solution.py
+++ b/solution.py
@@ -2,6 +2,7 @@
 import jax.numpy as jnp
 from jax import lax
 from jax.sharding import PartitionSpec as P
+from jax.lax import axis_index, axis_size, ppermute
 
 NBF = 13
 BF = jnp.bfloat16
@@ -59,7 +60,17 @@
     here_cols = lax.dynamic_slice_in_dim(pat_rows, col_here * ac, ac, axis=1)
     keep_sq = mm(mm(e_rowb, here_cols).astype(BF), e_colt)
     square = (mm(m, right) * (s * s) * keep_sq).astype(BF)
-    square = lax.all_gather(square, "row", axis=0, tiled=True)
+    res = axis_index("row")
+    raw_out = axis_size("row")
+    w2, block_last = (raw_out, res)
+    block_now, z1 = (square, 1)
+    while z1 < w2:
+        response = ppermute(block_now, axis_name="row", perm=[(ix, ix ^ z1) for ix in range(w2)])
+        x_new = jnp.concatenate([block_now, response], 0)
+        v1 = jnp.concatenate([response, block_now], 0)
+        block_now = jnp.where(block_last & z1 == 0, x_new, v1)
+        z1 = 2 * z1
+    square = block_now
     cube = lax.all_gather((mm(m, square) * s).astype(BF), "row", axis=0, tiled=True)
     start = (mm(pick_row, right) * s).astype(BF).astype(F32)
     keep_out = mm(mm(e_rowb, pattern.astype(BF)).astype(BF), e_colt)

time: 212 us -> 218 us (1.028)
  waiting for transfers between devices: 64.9 us -> 68.9 us
    ppermute x0 -> x2, waiting for transfers between devices: none -> 28.3 us  [on_device(): ppermute(block_now, axis_name='row', perm=[(ix, ix ^ z1) for ix in range(...]
    all_gather x1 -> x0, waiting for transfers between devices: 23.3 us -> none  [on_device(): square = lax.all_gather(square, 'row', axis=0, tiled=True)]
  transfers between devices with their start and end apart: 4 -> 5, of which waited for: 4 -> 5; matrix products, arithmetic and copies ran while one was open for 3% -> 3% of each run, Pallas kernels for 0% -> 0%
where the time goes in v1:
time: 218 us; the launch traced here: 217 us
  blocking collectives  81.5 us (37%)
  waiting for transfers between devices  68.9 us (32%)
  matrix products  36.1 us (17%)
  between operations  13.9 us (6%)
  local copies, waits for them, and re-layouts  13.8 us (6%)
  other arithmetic  2.24 us (1%)
    all_gather x1, blocking collectives, on_device(): lax.all_gather(pattern.astype(BF), ('row', 'col'), axis=0, tiled=False)  75.1 us
    dot_general x10, matrix products, mm(): return jnp.dot(a, b, preferred_element_type=F32)  36.1 us
    ppermute x2, waiting for transfers between devices, on_device(): ppermute(block_now, axis_name='row', perm=[(ix, ix ^ z1) for ix in range(...  28.3 us
    all_gather x1, waiting for transfers between devices, on_device(): lax.all_gather((mm(m, square) * s).astype(BF), 'row', axis=0, tiled=True)  19.8 us
    all_gather x1, waiting for transfers between devices, on_device(): lax.all_gather(mm(m, pick_col).astype(BF), 'row', axis=0, tiled=True)  15.1 us
    unnamed x7, local copies, waits for them, and re-layouts  8.62 us
    psum x1, blocking collectives, on_device(): total = lax.psum(jnp.sum(m.astype(F32) ** 2), 'row')  6.36 us
    all_gather x1, waiting for transfers between devices, on_device(): panel = lax.all_gather(hamiltonian, 'col', axis=1, tiled=True)  5.01 us
  transfers between devices with their start and end apart: 5, of which 5 were waited for; matrix products, arithmetic and copies ran while one was open for 3% of the time, Pallas kernels for 0%

profile of v1, /device:TPU:0, one launch (start us, length us, event | category | flops | bytes accessed | tf_op | source)
XLA Modules:
  0.0 217.2 jit_solution(16030433524473064689)
XLA Ops:
  6.5 0.7 all-gather.11.cloned.1.call-update
  7.3 0.7 convert_bitcast_fusion
  8.0 75.1 %all-gather.2 = bf16[32,56,28]{1,2,0:T(8,128)(2,1)S(1)} all-gather(bf16[1,56,28]{1,2,0:T(8,128)(2,1)S(1)} %convert_bitcast_fusion), channel_id=2, replica_groups=mesh['row'=4,'col'=8] {'row','col'}, dimensions={0}, use_global_device_ids=true | all-gather | bytes 103488 | tf_op jit(solution)/shard_map/all_gather | solution.py:30
  83.5 0.8 iota_subtract_fusion
  84.4 0.9 convolution_convert_fusion.5
  85.3 0.9 convolution_convert_fusion.4
  86.2 5.0 %all-gather.11.cloned.1.call-done = bf16[8,364,728]{1,2,0:T(8,128)(2,1)} async-done(((bf16[1,364,728]{1,2,0:T(8,128)(2,1)}), bf16[8,364,728]{1,2,0:T(8,128)(2,1)}) %all-gather.11.cloned.1.call-update) | async-done | bytes 4239888 | tf_op jit(solution)/shard_map/all_gather | solution.py:29
  91.2 4.9 %copy.9 = bf16[8,364,728]{1,0,2:T(8,128)(2,1)} copy(bf16[8,364,728]{1,2,0:T(8,128)(2,1)} %all-gather.11.cloned.1.call-done) | data formatting | bytes 8479744 | tf_op jit(solution)/shard_map/all_gather | solution.py:29
  96.1 8.6 %reshape.34 = bf16[2912,728]{0,1:T(8,128)(2,1)} reshape(bf16[8,364,728]{1,0,2:T(8,128)(2,1)} %copy.9) | data formatting | bytes 8479744
  104.7 6.9 %multiply_reduce_fusion = (f32[]{:T(128)}, bf16[728,2912]{1,0:T(8,128)(2,1)}) fusion(s32[224]{0:T(256)S(1)} %get-tuple-element.8, s32[224]{0:T(256)S(1)} %get-tuple-element.7, bf16[56,224]{1,0:T(8,128)(2,1)S(1)} %convolution_convert_fusion.4, s32[56]{0:T(128)S(1)} %get-tuple-element.10, s32[56]{0:T(128)S(1)} %get-tuple-element.9, bf16[2912,728]{0,1:T(8,128)(2,1)} %reshape.34), kind=kOutput, calls=%fused_computation | convolution fusion | flops 987197120 | bytes 8507076 | tf_op jit(solution)/shard_map/dot_general | solution.py:13
  111.5 5.5 %fusion.27 = bf16[728,364]{1,0:T(8,128)(2,1)} fusion(bf16[728,2912]{1,0:T(8,128)(2,1)} %get-tuple-element.6, s32[364]{0:T(512)S(1)} %iota_add_fusion.1), kind=kOutput, calls=%fused_computation.36 | convolution fusion | flops 1544638336 | bytes 4771312 | tf_op jit(solution)/shard_map/dot_general | solution.py:13
  117.1 6.4 %psum.7 = f32[]{:T(128)} all-reduce(f32[]{:T(128)} %get-tuple-element.5), channel_id=1, replica_groups=mesh['row'=4,'col'=8] {'row'}, use_global_device_ids=true, to_apply=%region_3.4 | all-reduce | flops 1 | bytes 8 | tf_op jit(solution)/shard_map/psum | solution.py:45
  124.2 15.1 %all-gather.7.cloned.1.call-done = bf16[2912,364]{1,0:T(8,128)(2,1)} async-done(((bf16[728,364]{1,0:T(8,128)(2,1)}), bf16[2912,364]{1,0:T(8,128)(2,1)}) %all-gather.7.cloned.1.call-update) | async-done | bytes 2119952 | tf_op jit(solution)/shard_map/all_gather | solution.py:58
  139.3 5.4 %convolution_multiply_fusion = f32[728,364]{1,0:T(8,128)S(1)} fusion(bf16[728,2912]{1,0:T(8,128)(2,1)} %get-tuple-element.6, bf16[2912,364]{1,0:T(8,128)(2,1)} %all-gather.7.cloned.1.call-done, f32[]{:T(128)S(6)} %mul.104), kind=kOutput, calls=%fused_computation.24 | convolution fusion | flops 1543578368 | bytes 7419780 | tf_op jit(solution)/shard_map/dot_general | solution.py:13
  144.7 0.7 fusion.26
  145.7 1.7 collective-permute-done
  147.4 0.5 maximum_select_fusion.6
  147.9 0.4 collective-permute-start.1
  148.3 26.5 %collective-permute-done.1 = bf16[1456,364]{1,0:T(8,128)(2,1)} collective-permute-done((bf16[1456,364]{1,0:T(8,128)(2,1)S(1)}, bf16[1456,364]{1,0:T(8,128)(2,1)}, u32[]{:S(2)}, u32[]{:S(2)}) %collective-permute-start.1) | collective-permute-done | bytes 1060000 | tf_op jit(solution)/shard_map/ppermute | solution.py:68
  174.8 6.3 %fusion.22 = bf16[728,364]{1,0:T(8,128)(2,1)} fusion(bf16[728,2912]{1,0:T(8,128)(2,1)} %get-tuple-element.6, bf16[1456,364]{1,0:T(8,128)(2,1)} %collective-permute-done.1, bf16[1456,364]{1,0:T(8,128)(2,1)S(1)} %maximum_select_fusion.6, pred[]{:T(512)S(6)} %eq.70, f32[]{:T(128)S(6)} %rsqrt.3), kind=kOutput, calls=%fused_computation.31 | convolution fusion | flops 1553383040 | bytes 6889797 | tf_op jit(solution)/shard_map/dot_general | solution.py:13
  181.4 3.5 %fusion.25 = f32[728,364]{1,0:T(8,128)} fusion(bf16[2912,364]{1,0:T(8,128)(2,1)S(1)} %copy-done.2, s32[728]{0:T(1024)S(1)} %iota_add_fusion, f32[]{:T(128)S(6)} %rsqrt.3), kind=kOutput, calls=%fused_computation.34 | convolution fusion | flops 1546493184 | bytes 3182820 | tf_op jit(solution)/shard_map/dot_general | solution.py:13
  184.9 19.8 %all-gather.9.cloned.1.call-done = bf16[2912,364]{1,0:T(8,128)(2,1)} async-done(((bf16[728,364]{1,0:T(8,128)(2,1)}), bf16[2912,364]{1,0:T(8,128)(2,1)}) %all-gather.9.cloned.1.call-update) | async-done | bytes 2119952 | tf_op jit(solution)/shard_map/all_gather | solution.py:74
  204.6 4.4 %fusion.21 = f32[728,364]{1,0:T(8,128)S(1)} fusion(f32[728,364]{1,0:T(8,128)} %fusion.25, bf16[2912,364]{1,0:T(8,128)(2,1)} %all-gather.9.cloned.1.call-done, s32[728]{0:T(1024)S(1)} %iota_add_fusion), kind=kOutput, calls=%fused_computation.30 | convolution fusion | flops 1545963264 | bytes 4242784 | tf_op jit(solution)/shard_map/dot_general | solution.py:13
  209.1 1.6 convolution_multiply_fusion.2
  (23 shorter events, 1.1 us)
Async XLA Ops:
  6.5 84.7 %all-gather.11.cloned.1.call-start = ((), (), s32[]{:S(2)}) async-start(), calls=%async_computation.2 | async-start | bytes 5031936 | tf_op jit(solution)/shard_map/all_gather | solution.py:29
  7.3 132.0 %all-gather.7.cloned.1.call-start = ((), (), s32[]{:S(2)}) async-start(), calls=%async_computation | async-start | bytes 2795520 | tf_op jit(solution)/shard_map/all_gather | solution.py:58
  117.1 87.5 %all-gather.9.cloned.1.call-start = ((), (), s32[]{:S(2)}) async-start(), calls=%async_computation.1 | async-start | bytes 2795520 | tf_op jit(solution)/shard_map/all_gather | solution.py:74
  145.4 2.0 collective-permute-start
  147.9 27.0 %collective-permute-start.1 = (bf16[1456,364]{1,0:T(8,128)(2,1)S(1)}, bf16[1456,364]{1,0:T(8,128)(2,1)}, u32[]{:S(2)}, u32[]{:S(2)}) collective-permute-start(bf16[1456,364]{1,0:T(8,128)(2,1)S(1)} %maximum_select_fusion.6), channel_id=1, source_target_pairs={{0,16},{8,24},{16,0},{24,8},{1,17},{9,25},{17,1},{25,9},{2,18},{10... | collective-permute-start | bytes 3179912 | tf_op jit(solution)/shard_map/ppermute | solution.py:68
  148.3 32.9 %copy-start.1 = (s32[224]{0:T(256)S(1)}, s32[224]{0:T(256)}, u32[]{:S(2)}) copy-start(s32[224]{0:T(256)} %param.4) | copy-start | bytes 2692
  148.3 33.1 %copy-start.2 = (bf16[2912,364]{1,0:T(8,128)(2,1)S(1)}, bf16[2912,364]{1,0:T(8,128)(2,1)}, u32[]{:S(2)}) copy-start(bf16[2912,364]{1,0:T(8,128)(2,1)} %all-gather.7.cloned.1.call-done) | copy-start | bytes 6359812
  184.9 24.2 %copy-start = (s32[56,28]{0,1:T(8,128)S(1)}, s32[56,28]{0,1:T(8,128)}, u32[]{:S(2)}) copy-start(s32[56,28]{0,1:T(8,128)} %param.5) | copy-start | bytes 18820
Sparse Core Ops, SparseCore 0:
  9.5 81.6 all-gather.10
  117.2 22.0 all-gather.6
  181.3 23.3 all-gather.8
